TPU v7x, 256 devices: a whole 4x4x8 slice. The times are simulated.
256 devices in a mesh: ctx: 8 (over z), exp: 32 (over x, y, core).
Axes of the slice: x: 4, y: 4, z: 8, core: 2. Of those that a mesh axis runs over, the one named last changes fastest.
Arguments:
- q_latent: bfloat16 [128, 128, 512], P('exp'), may hold values from -7 to 7
- q_rope: bfloat16 [128, 64, 128], P('exp'), may hold values from -84 to 84
- cache_latent: bfloat16 [128, 4096, 512], P('exp', 'ctx'), may hold values from -6 to 6
- cache_rope: bfloat16 [128, 64, 4096], P('exp', None, 'ctx'), may hold values from -6 to 6
- lengths: int32 [128], P('exp'), may hold values from 1024 to 4096
- w_attn_out: bfloat16 [128, 512, 7168], P('ctx', None, 'exp'), may hold values from -0.1875 to 0.1875
- hidden_in: bfloat16 [128, 7168], P(None, 'exp'), may hold values from -6 to 6
- norm_gain: bfloat16 [7168], replicated, may hold values from 0.5 to 8
- w_gate: bfloat16 [32, 7168, 1024], P('exp', None, 'ctx'), may hold values from -0.0625 to 0.0625
- w_up: bfloat16 [32, 7168, 1024], P('exp', None, 'ctx'), may hold values from -0.0625 to 0.0625
- w_down: bfloat16 [32, 1024, 7168], P('exp', 'ctx'), may hold values from -0.1875 to 0.1875
- expert_ids: int32 [128, 8], replicated, may hold values from 0 to 31, all different within a row; in each aligned block of 128 rows (0 to 127, 128 to 255, ...) at most 64 rows name the same one
- gate_weights: float32 [128, 8], replicated, may hold values from 0.1 to 1
Outputs:
- layer_out: bfloat16 [128, 7168], P('exp', 'ctx')
Inputs may be any that keep to these rules, and one draw needn't show every extreme that they name: `expert_ids`: each row names 8 different experts; over all 128 rows no expert is named more than 64 times, a bound that some block reaches.
All inputs are finite; a program needn't handle non-finite values.
Results may differ from a plain program's by a relative error of at most 0.008.
Values may be sent and summed in bfloat16 or wider, within the bound.
A program may use at most 64 MiB of HBM per device.

v0:
```python
import math
import jax
import jax.numpy as jnp
from jax import lax
from jax.sharding import PartitionSpec as P

SOFTMAX_SCALE = 192.0 ** (-0.5)
MASKED = -1e30
EPSILON = 1e-06


def cut_along(array, dim, devices):
    before, after = (array.shape[:dim], array.shape[dim + 1 :])
    return jnp.moveaxis(array.reshape(*before, devices, -1, *after), dim, 0)


def summed_on_arrival(array, axis, dim):
    devices = lax.axis_size(axis)
    blocks = lax.all_to_all(cut_along(array, dim, devices), axis, 0, 0, tiled=True)
    return jnp.sum(blocks, axis=0)


def sent_together(arrays, axis, dim, along):
    widths = [math.prod(a.shape[along:]) for a in arrays]
    both = jnp.concatenate(
        [a.reshape(*a.shape[:along], w) for a, w in zip(arrays, widths)], axis=along
    )
    filled = summed_on_arrival(both, axis, dim)
    blocks = jnp.split(filled, [sum(widths[:k]) for k in range(1, len(widths))], axis=along)
    return tuple(
        (b.reshape(*filled.shape[:along], *a.shape[along:]) for a, b in zip(arrays, blocks))
    )


def copy_for_each(array, axis):
    copies = jnp.broadcast_to(array, (lax.axis_size(axis), *array.shape))
    return lax.all_to_all(copies, axis, split_axis=0, concat_axis=0, tiled=True)


def taken_together(array, axis):
    everything = copy_for_each(array, axis)
    return jnp.sum(everything, axis=0)


def slot_tables(expert_ids, gate_weights, experts, capacity):
    row_count, top_count = expert_ids.shape
    flat_ids = expert_ids.reshape(-1)
    one_hot = (flat_ids[:, None] == jnp.arange(experts, dtype=jnp.int32)[None, :]).astype(jnp.int32)
    before = jnp.cumsum(one_hot, axis=0) - one_hot
    slot_index = jnp.sum(before * one_hot, axis=1)
    target = flat_ids * capacity + slot_index
    owner_row = jnp.arange(row_count * top_count, dtype=jnp.int32) // top_count
    slot_row = jnp.full((experts * capacity,), row_count, jnp.int32).at[target].set(owner_row)
    slot_gate = (
        jnp.zeros((experts * capacity,), jnp.float32).at[target].set(gate_weights.reshape(-1))
    )
    return (slot_row, slot_gate)


def per_device(
    q_latent,
    q_rope,
    cache_latent,
    cache_rope,
    lengths,
    w_attn_out,
    hidden_in,
    norm_gain,
    w_gate,
    w_up,
    w_down,
    expert_ids,
    gate_weights,
):
    ctx_index = lax.axis_index("ctx")
    exp_index = lax.axis_index("exp")
    ctx_count = lax.axis_size("ctx")
    exp_count = lax.axis_size("exp")
    block_len = cache_latent.shape[1]
    positions = ctx_index * block_len + jnp.arange(block_len, dtype=jnp.int32)
    visible = positions[None, :] < lengths[:, None]
    scores = jnp.einsum("rhl,rpl->rhp", q_latent, cache_latent, preferred_element_type=jnp.float32)
    scores = (
        scores + jnp.einsum("rdh,rdp->rhp", q_rope, cache_rope, preferred_element_type=jnp.float32)
    ) * SOFTMAX_SCALE
    scores = jnp.where(visible[:, None, :], scores, MASKED)
    block_max = jnp.max(scores, axis=2)
    weights = jnp.where(visible[:, None, :], jnp.exp(scores - block_max[..., None]), 0.0)
    block_total = jnp.sum(weights, axis=2)
    block_value = jnp.einsum(
        "rhp,rpl->rhl",
        weights.astype(jnp.bfloat16),
        cache_latent,
        preferred_element_type=jnp.float32,
    )
    head_count = w_attn_out.shape[0]
    joint_max = lax.pmax(block_max, "ctx")
    rescale = jnp.exp(block_max - joint_max)
    share_total, share_value = sent_together(
        (block_total * rescale, block_value * rescale[..., None]), "ctx", 1, 2
    )
    attended = (share_value / share_total[..., None]).astype(jnp.bfloat16)
    latent_width = w_attn_out.shape[1]
    flat_weight = w_attn_out.reshape(head_count * latent_width, w_attn_out.shape[2])
    row_piece = lax.all_gather(attended, "exp", axis=0, tiled=True)
    partial_out = jnp.dot(
        row_piece.reshape(row_piece.shape[0], head_count * latent_width),
        flat_weight,
        preferred_element_type=jnp.float32,
    )
    hidden_state = hidden_in.astype(jnp.float32) + taken_together(partial_out, "ctx")
    row_count = hidden_in.shape[0]
    share_width = hidden_in.shape[1]
    model_width = share_width * exp_count
    column_width = model_width // ctx_count
    top_count = expert_ids.shape[1]
    local_experts = w_gate.shape[0]
    experts = exp_count * local_experts
    capacity = min(row_count, 2 * row_count * top_count // experts)
    slot_row, slot_gate = slot_tables(expert_ids, gate_weights, experts, capacity)
    rounded = hidden_state.astype(jnp.bfloat16)
    padded = jnp.concatenate([rounded, jnp.zeros((1, share_width), jnp.bfloat16)], axis=0)
    outbound = padded[slot_row].reshape(experts, capacity, share_width)
    values = lax.all_to_all(outbound, "exp", split_axis=0, concat_axis=2, tiled=True).astype(
        jnp.float32
    )
    mean_square = jnp.mean(values * values, axis=2, keepdims=True)
    normed = (values * lax.rsqrt(mean_square + EPSILON) * norm_gain.astype(jnp.float32)).astype(
        jnp.bfloat16
    )
    gate_part = jnp.einsum("end,edf->enf", normed, w_gate, preferred_element_type=jnp.float32)
    up_part = jnp.einsum("end,edf->enf", normed, w_up, preferred_element_type=jnp.float32)
    active = (jax.nn.silu(gate_part) * up_part).astype(jnp.bfloat16)
    expert_part = jnp.einsum("enf,efd->end", active, w_down, preferred_element_type=jnp.float32)
    local_rows = lax.dynamic_slice_in_dim(
        slot_row, exp_index * local_experts * capacity, local_experts * capacity
    )
    local_gates = lax.dynamic_slice_in_dim(
        slot_gate, exp_index * local_experts * capacity, local_experts * capacity
    )
    weighted = expert_part.reshape(local_experts * capacity, model_width) * local_gates[:, None]
    owner_block = exp_index * share_width // column_width
    offset = exp_index * share_width % column_width
    column_part = summed_on_arrival(weighted, "ctx", 1)
    summed = jax.ops.segment_sum(column_part, local_rows, num_segments=row_count)
    current = lax.dynamic_slice(summed, (0, offset), (row_count, share_width))
    residual = jnp.where(ctx_index == owner_block, hidden_state, 0.0)
    summed = lax.dynamic_update_slice(summed, current + residual, (0, offset))
    layer_out = summed_on_arrival(summed, "exp", 0)
    return layer_out.astype(jnp.bfloat16)


def solution(mesh):
    in_specs = (
        P("exp", None, None),
        P("exp", None, None),
        P("exp", "ctx", None),
        P("exp", None, "ctx"),
        P("exp"),
        P("ctx", None, "exp"),
        P(None, "exp"),
        P(),
        P("exp", None, "ctx"),
        P("exp", None, "ctx"),
        P("exp", "ctx", None),
        P(),
        P(),
    )
    out_specs = P("exp", "ctx")
    return jax.shard_map(
        per_device, mesh=mesh, in_specs=in_specs, out_specs=out_specs, check_vma=False
    )
```

profile of v0, /device:TPU:1, one launch (start us, length us, event | category | flops | bytes accessed | tf_op | source)
XLA Modules:
  0.0 277.0 jit_solution(6442682698349328505)
XLA Ops:
  8.1 1.9 fusion.58
  10.5 17.3 %pmax.7 = f32[4,128]{1,0:T(4,128)S(1)} all-reduce(f32[4,128]{1,0:T(4,128)S(1)} %get-tuple-element.7), channel_id=1, replica_groups=mesh['ctx'=8,'exp'=32] {'ctx'}, use_global_device_ids=true, to_apply=%region_6.7 | all-reduce | flops 512 | bytes 4096 | tf_op jit(solution)/shard_map/pmax | solution.py:97
  30.0 1.6 maximum_bitcast_fusion
  31.7 31.7 %all_to_all.29 = f32[8,4,16,513]{3,2,1,0:T(8,128)S(1)} all-to-all(f32[8,4,16,513]{3,2,1,0:T(8,128)S(1)} %maximum_bitcast_fusion), channel_id=1, replica_groups=mesh['ctx'=8,'exp'=32] {'ctx'}, dimensions={0} | all-to-all | bytes 2101248 | tf_op jit(solution)/shard_map/all_to_all | solution.py:19
  64.9 1.6 fusion.37
  66.6 51.4 %all-gather.2.cloned.1.call-done = bf16[128,16,512]{2,1,0:T(8,128)(2,1)} async-done(((bf16[4,16,512]{2,1,0:T(8,128)(2,1)}), bf16[128,16,512]{2,1,0:T(8,128)(2,1)}) %all-gather.2.cloned.1.call-update) | async-done | bytes 2097168 | tf_op jit(solution)/shard_map/all_gather | solution.py:105
  118.0 5.2 %fusion.11 = f32[128,224]{0,1:T(8,128)S(1)} fusion(bf16[16,512,224]{1,2,0:T(8,128)(2,1)} %param.18, bf16[128,16,512]{2,1,0:T(8,128)(2,1)} %all-gather.2.cloned.1.call-done), kind=kOutput, calls=%fused_computation.21 | convolution fusion | flops 469762048 | bytes 5881856 | tf_op jit(solution)/shard_map/dot_general | solution.py:106
  124.2 6.7 %all-to-all-start.1 = ((f32[8,128,224]{1,2,0:T(8,128)}), f32[8,128,224]{1,2,0:T(8,128)S(1)}, u32[]{:S(2)}, u32[]{:S(2)}) async-start(f32[8,128,224]{1,2,0:T(8,128)} %broadcast_in_dim.59), calls=%async_computation.1 | async-start | bytes 1835008 | tf_op jit(solution)/shard_map/all_to_all | solution.py:37
  131.6 9.0 %reduce-window.6 = s32[32,8,128]{2,1,0:T(8,128)S(1)} reduce-window(s32[32,8,128]{2,1,0:T(8,128)S(1)} %fusion.38, s32[]{:T(128)} %constant.34.clone.1), window={size=1x1x128 pad=0_0x0_0x127_0}, to_apply=%region_0.1 | reduce-window | flops 4161536 | bytes 262148 | tf_op jit(solution)/shard_map/reduce-window
  141.1 4.3 %scatter_custom_fusion = s32[2048]{0:T(1024)S(1)} fusion(s32[1024]{0:T(1024)S(1)} %bitcast.76, s32[1024]{0:T(1024)S(1)} %add_select_fusion, s32[]{:T(128)} %constant.31.clone.1), kind=kCustom, calls=%fused_computation.66 | custom fusion | bytes 8196 | tf_op jit(solution)/shard_map/scatter | solution.py:53
  145.5 11.9 %all-to-all-done.1 = f32[8,128,224]{1,2,0:T(8,128)S(1)} async-done(((f32[8,128,224]{1,2,0:T(8,128)}), f32[8,128,224]{1,2,0:T(8,128)S(1)}, u32[]{:S(2)}, u32[]{:S(2)}) %all-to-all-start.1) | async-done | bytes 917536 | tf_op jit(solution)/shard_map/all_to_all | solution.py:37
  157.5 9.0 %gather_fusion = bf16[2048,224]{1,0:T(8,128)(2,1)} fusion(bf16[129,224]{1,0:T(8,128)(2,1)S(1)} %concatenate.14, s32[2048]{0:T(1024)S(1)} %fusion.46), kind=kCustom, calls=%fused_computation | custom fusion | bytes 1843200 | tf_op jit(solution)/shard_map/gather | solution.py:123
  166.5 5.6 %all-to-all-start.2 = ((bf16[32,64,224]{2,1,0:T(8,128)(2,1)}), bf16[32,64,224]{2,1,0:T(8,128)(2,1)S(1)}, u32[]{:S(2)}, u32[]{:S(2)}) async-start(bf16[32,64,224]{2,1,0:T(8,128)(2,1)} %bitcast.71), calls=%async_computation.2 | async-start | bytes 2097152 | tf_op jit(solution)/shard_map/all_to_all | solution.py:124
  172.4 4.5 %scatter_custom_fusion.1 = f32[2048]{0:T(1024)S(1)} fusion(s32[1024]{0:T(1024)S(1)} %bitcast.77, f32[1024]{0:T(1024)S(1)} %reshape.230, f32[]{:T(128)} %constant.28.clone.1), kind=kCustom, calls=%fused_computation.63 | custom fusion | bytes 8196 | tf_op jit(solution)/shard_map/scatter | solution.py:55
  176.9 3.9 %copy.72 = bf16[7168,128]{1,0:T(8,128)(2,1)} copy(bf16[7168,128]{0,1:T(8,128)(2,1)} %bitcast.72) | data formatting | bytes 3670016 | tf_op jit(solution)/shard_map/enf,efd->end/dot_general | solution.py:134
  180.9 8.1 %all-to-all-done.2 = bf16[32,64,224]{2,1,0:T(8,128)(2,1)S(1)} async-done(((bf16[32,64,224]{2,1,0:T(8,128)(2,1)}), bf16[32,64,224]{2,1,0:T(8,128)(2,1)S(1)}, u32[]{:S(2)}, u32[]{:S(2)}) %all-to-all-start.2) | async-done | bytes 917536 | tf_op jit(solution)/shard_map/all_to_all | solution.py:124
  189.7 1.6 copy.69
  191.3 2.6 convert_element_type.70
  193.9 2.0 fusion.7
  195.9 4.5 %multiply_bitcast_fusion = f32[8,64,896]{2,1,0:T(8,128)} fusion(bf16[8,896,128]{2,1,0:T(8,128)(2,1)} %bitcast.69, f32[64]{0:T(128)S(1)} %dynamic_slice.10, bf16[64,7168]{1,0:T(8,128)(2,1)S(1)} %convert_element_type.70, bf16[1,7168,128]{2,1,0:T(8,128)(2,1)} %param.22, f32[64,128]{1,0:T(8,128)S(1)} %fusion.7), kind=kOutput, calls=%fused_computation.15 | convolution fusion | flops 235388928 | bytes 6455552 | tf_op jit(solution)/shard_map/enf,efd->end/dot_general | solution.py:134
  200.4 4.3 %all-to-all-start.3 = ((f32[8,64,896]{2,1,0:T(8,128)}), f32[8,64,896]{2,1,0:T(8,128)}, u32[]{:S(2)}, u32[]{:S(2)}) async-start(f32[8,64,896]{2,1,0:T(8,128)} %multiply_bitcast_fusion), calls=%async_computation.3 | async-start | bytes 3670016 | tf_op jit(solution)/shard_map/all_to_all | solution.py:19
  204.8 43.0 %all-to-all-done.3 = f32[8,64,896]{2,1,0:T(8,128)} async-done(((f32[8,64,896]{2,1,0:T(8,128)}), f32[8,64,896]{2,1,0:T(8,128)}, u32[]{:S(2)}, u32[]{:S(2)}) %all-to-all-start.3) | async-done | bytes 1835040 | tf_op jit(solution)/shard_map/all_to_all | solution.py:19
  247.8 1.6 reduce_sum.71
  252.2 17.2 %all_to_all.30 = f32[32,4,896]{2,1,0:T(4,128)S(1)} all-to-all(f32[32,4,896]{2,1,0:T(4,128)S(1)} %reshape.207), channel_id=1, replica_groups=mesh['ctx'=8,'exp'=32] {'exp'}, dimensions={0} | all-to-all | bytes 917504 | tf_op jit(solution)/shard_map/all_to_all | solution.py:19
  (62 shorter events, 12.7 us)
Async XLA Ops:
  6.5 1.6 copy-start
  6.5 111.4 %all-gather.2.cloned.1.call-start = ((), (), s32[]{:S(2)}) async-start(), calls=%async_computation.5 | async-start | bytes 2162688 | tf_op jit(solution)/shard_map/all_gather | solution.py:105
  8.1 1.9 copy-start.1
  8.1 1.9 copy-start.2
  123.2 7.7 %copy-start.4 = (s32[128,8]{0,1:T(8,128)S(1)}, s32[128,8]{0,1:T(8,128)}, u32[]{:S(2)}) copy-start(s32[128,8]{0,1:T(8,128)} %param.24) | copy-start | bytes 12292
  123.2 8.2 %copy-start.3 = (bf16[128,224]{0,1:T(8,128)(2,1)S(1)}, bf16[128,224]{0,1:T(8,128)(2,1)}, u32[]{:S(2)}) copy-start(bf16[128,224]{0,1:T(8,128)(2,1)} %param.19) | copy-start | bytes 172036
  124.2 33.1 %all-to-all-start.1 = ((f32[8,128,224]{1,2,0:T(8,128)}), f32[8,128,224]{1,2,0:T(8,128)S(1)}, u32[]{:S(2)}, u32[]{:S(2)}) async-start(f32[8,128,224]{1,2,0:T(8,128)} %broadcast_in_dim.59), calls=%async_computation.1 | async-start | bytes 1835008 | tf_op jit(solution)/shard_map/all_to_all | solution.py:37
  166.5 5.6 %copy-start.5 = (bf16[7168]{0:T(1024)(128)(2,1)S(1)}, bf16[7168]{0:T(1024)(128)(2,1)}, u32[]{:S(2)}) copy-start(bf16[7168]{0:T(1024)(128)(2,1)} %param.20) | copy-start | bytes 43012
  166.5 5.7 %copy-start.6 = (f32[128,8]{0,1:T(8,128)S(1)}, f32[128,8]{0,1:T(8,128)}, u32[]{:S(2)}) copy-start(f32[128,8]{0,1:T(8,128)} %param.25) | copy-start | bytes 12292
  166.5 22.5 %all-to-all-start.2 = ((bf16[32,64,224]{2,1,0:T(8,128)(2,1)}), bf16[32,64,224]{2,1,0:T(8,128)(2,1)S(1)}, u32[]{:S(2)}, u32[]{:S(2)}) async-start(bf16[32,64,224]{2,1,0:T(8,128)(2,1)} %bitcast.71), calls=%async_computation.2 | async-start | bytes 2097152 | tf_op jit(solution)/shard_map/all_to_all | solution.py:124
  200.4 47.5 %all-to-all-start.3 = ((f32[8,64,896]{2,1,0:T(8,128)}), f32[8,64,896]{2,1,0:T(8,128)}, u32[]{:S(2)}, u32[]{:S(2)}) async-start(f32[8,64,896]{2,1,0:T(8,128)} %multiply_bitcast_fusion), calls=%async_computation.3 | async-start | bytes 3670016 | tf_op jit(solution)/shard_map/all_to_all | solution.py:19
Sparse Core Ops, SparseCore 0:
  66.7 51.2 all-gather.1
where the time goes:
time: 278 us; the launch traced here: 277 us
  waiting for transfers between devices  114 us (41%)
  blocking collectives  66.1 us (24%)
  local copies, waits for them, and re-layouts  31.7 us (11%)
  other arithmetic  18.8 us (7%)
  starting transfers between devices  16.6 us (6%)
  matrix products  15.6 us (6%)
  between operations  13.7 us (5%)
    all_gather x1, waiting for transfers between devices, per_device(): row_piece = lax.all_gather(attended, 'exp', axis=0, tiled=True)  51.4 us
    all_to_all x2, blocking collectives, summed_on_arrival(): lax.all_to_all(cut_along(array, dim, devices), axis, 0, 0, tiled=True)  48.9 us
    all_to_all x1, waiting for transfers between devices, summed_on_arrival(): lax.all_to_all(cut_along(array, dim, devices), axis, 0, 0, tiled=True)  43 us
    pmax x1, blocking collectives, per_device(): joint_max = lax.pmax(block_max, 'ctx')  17.3 us
    all_to_all x1, waiting for transfers between devices, copy_for_each(): return lax.all_to_all(copies, axis, split_axis=0, concat_axis=0, tiled=True)  11.9 us
    another operation x3, other arithmetic  9.15 us
    gather x1, local copies, waits for them, and re-layouts, per_device(): outbound = padded[slot_row].reshape(experts, capacity, share_width)  9 us
    all_to_all x1, waiting for transfers between devices, per_device(): lax.all_to_all(outbound, 'exp', split_axis=0, concat_axis=2, tiled=True)  8.11 us
  transfers between devices with their start and end apart: 4, of which 4 were waited for; matrix products, arithmetic and copies ran while one was open for 8% of the time, Pallas kernels for 0%

commit v1 on v0

--- a/solution.py
+++ b/solution.py
@@ -7,6 +7,26 @@
 SOFTMAX_SCALE = 192.0 ** (-0.5)
 MASKED = -1e30
 EPSILON = 1e-06
+
+
+def build_entries_on(state, pos_dim):
+    built = list(state.shape[1:])
+    built[pos_dim] *= state.shape[0]
+    return jnp.moveaxis(state, 0, pos_dim).reshape(built)
+
+
+def build_sums_all_for(slab_in, bus_axis):
+    block_now = lax.axis_size(bus_axis)
+    t1, shaped = (block_now, lax.axis_index(bus_axis))
+    g_now, x_new = (slab_in[None], 1)
+    while x_new < t1:
+        met_up = lax.ppermute(g_now, bus_axis, [(p, p ^ x_new) for p in range(t1)])
+        piece_next = shaped & x_new == 0
+        g_now = jnp.concatenate(
+            [jnp.where(piece_next, g_now, met_up), jnp.where(piece_next, met_up, g_now)]
+        )
+        x_new *= 2
+    return g_now
 
 
 def cut_along(array, dim, devices):
@@ -102,7 +122,11 @@
     attended = (share_value / share_total[..., None]).astype(jnp.bfloat16)
     latent_width = w_attn_out.shape[1]
     flat_weight = w_attn_out.reshape(head_count * latent_width, w_attn_out.shape[2])
-    row_piece = lax.all_gather(attended, "exp", axis=0, tiled=True)
+
+    def _return_all_field(local, mine, dim_at):
+        return build_entries_on(build_sums_all_for(local, mine), dim_at)
+
+    row_piece = _return_all_field(attended, "exp", 0)
     partial_out = jnp.dot(
         row_piece.reshape(row_piece.shape[0], head_count * latent_width),
         flat_weight,

time: 278 us -> 270 us (0.971)
  starting transfers between devices: 16.6 us -> 34.1 us
  waiting for transfers between devices: 114 us -> 98.1 us
  between operations: 13.7 us -> 0.39 us
  other arithmetic: 18.8 us -> 23.2 us
  local copies, waits for them, and re-layouts: 31.7 us -> 36 us
  matrix products: 15.6 us -> 11.5 us
    all_gather x1 -> x0, waiting for transfers between devices: 51.4 us -> none  [per_device(): row_piece = lax.all_gather(attended, 'exp', axis=0, tiled=True)]
    ppermute x0 -> x5, waiting for transfers between devices: none -> 38.3 us  [build_sums_all_for(): met_up = lax.ppermute(g_now, bus_axis, [(p, p ^ x_new) for p in range(t1)])]
    ppermute x0 -> x5, starting transfers between devices: none -> 15.1 us  [build_sums_all_for(): met_up = lax.ppermute(g_now, bus_axis, [(p, p ^ x_new) for p in range(t1)])]
    all_to_all x1, starting transfers between devices: 5.58 us -> 11.1 us  [per_device(): lax.all_to_all(outbound, 'exp', split_axis=0, concat_axis=2, tiled=True)]
    dot_general x1, matrix products: 5.24 us -> 1.2 us  [per_device(): jnp.dot(row_piece.reshape(row_piece.shape[0], head_count * latent_width),...]
    select_n x0 -> x5, other arithmetic: none -> 3.63 us  [build_sums_all_for(): jnp.where(piece_next, g_now, met_up)]
    all_to_all x1, waiting for transfers between devices: 11.9 us -> 8.42 us  [copy_for_each(): return lax.all_to_all(copies, axis, split_axis=0, concat_axis=0, tiled=True)]
    all_to_all x1, starting transfers between devices: 6.73 us -> 3.55 us  [copy_for_each(): return lax.all_to_all(copies, axis, split_axis=0, concat_axis=0, tiled=True)]
  transfers between devices with their start and end apart: 4 -> 8, of which waited for: 4 -> 8; matrix products, arithmetic and copies ran while one was open for 8% -> 9% of each run, Pallas kernels for 0% -> 0%
where the time goes in v1:
time: 270 us; the launch traced here: 269 us
  waiting for transfers between devices  98.1 us (36%)
  blocking collectives  66.2 us (25%)
  local copies, waits for them, and re-layouts  36 us (13%)
  starting transfers between devices  34.1 us (13%)
  other arithmetic  23.2 us (9%)
  matrix products  11.5 us (4%)
    all_to_all x2, blocking collectives, summed_on_arrival(): lax.all_to_all(cut_along(array, dim, devices), axis, 0, 0, tiled=True)  48.9 us
    all_to_all x1, waiting for transfers between devices, summed_on_arrival(): lax.all_to_all(cut_along(array, dim, devices), axis, 0, 0, tiled=True)  43.1 us
    ppermute x5, waiting for transfers between devices, build_sums_all_for(): met_up = lax.ppermute(g_now, bus_axis, [(p, p ^ x_new) for p in range(t1)])  38.3 us
    pmax x1, blocking collectives, per_device(): joint_max = lax.pmax(block_max, 'ctx')  17.3 us
    ppermute x5, starting transfers between devices, build_sums_all_for(): met_up = lax.ppermute(g_now, bus_axis, [(p, p ^ x_new) for p in range(t1)])  15.1 us
    all_to_all x1, starting transfers between devices, per_device(): lax.all_to_all(outbound, 'exp', split_axis=0, concat_axis=2, tiled=True)  11.1 us
    another operation x3, other arithmetic  9.14 us
    gather x1, local copies, waits for them, and re-layouts, per_device(): outbound = padded[slot_row].reshape(experts, capacity, share_width)  9 us
  transfers between devices with their start and end apart: 8, of which 8 were waited for; matrix products, arithmetic and copies ran while one was open for 9% of the time, Pallas kernels for 0%

profile of v1, /device:TPU:1, one launch (start us, length us, event | category | flops | bytes accessed | tf_op | source)
XLA Modules:
  0.0 269.3 jit_solution(867560357957013200)
XLA Ops:
  3.9 17.3 %pmax.7 = f32[4,128]{1,0:T(4,128)S(1)} all-reduce(f32[4,128]{1,0:T(4,128)S(1)} %get-tuple-element.17), channel_id=1, replica_groups=mesh['ctx'=8,'exp'=32] {'ctx'}, use_global_device_ids=true, to_apply=%region_6.7 | all-reduce | flops 512 | bytes 4096 | tf_op jit(solution)/shard_map/pmax | solution.py:117
  25.1 31.7 %all_to_all.29 = f32[8,4,16,513]{3,2,1,0:T(8,128)S(1)} all-to-all(f32[8,4,16,513]{3,2,1,0:T(8,128)S(1)} %maximum_bitcast_fusion), channel_id=1, replica_groups=mesh['ctx'=8,'exp'=32] {'ctx'}, dimensions={0} | all-to-all | bytes 2101248 | tf_op jit(solution)/shard_map/all_to_all | solution.py:39
  59.3 6.7 %collective-permute-start = (bf16[1,4,16,512]{3,2,1,0:T(8,128)(2,1)S(1)}, bf16[1,4,16,512]{3,2,1,0:T(8,128)(2,1)S(1)}, u32[]{:S(2)}, u32[]{:S(2)}) collective-permute-start(bf16[1,4,16,512]{3,2,1,0:T(8,128)(2,1)S(1)} %fusion.35), channel_id=1, source_target_pairs={{0,1},{1,0},{2,3},{3,2},{4,5},{5,4},{6,7},{7,6},{8,9},{9,8},{10,11... | collective-permute-start | bytes 196616 | tf_op jit(solution)/shard_map/ppermute | solution.py:23
  69.4 3.4 %collective-permute-done.1 = bf16[2,4,16,512]{3,2,1,0:T(8,128)(2,1)S(1)} collective-permute-done((bf16[2,4,16,512]{3,2,1,0:T(8,128)(2,1)S(1)}, bf16[2,4,16,512]{3,2,1,0:T(8,128)(2,1)S(1)}, u32[]{:S(2)}, u32[]{:S(2)}) %collective-permute-start.1) | collective-permute-done | bytes 131104 | tf_op jit(solution)/shard_map/ppermute | solution.py:23
  72.8 3.0 %collective-permute-start.2 = (bf16[4,4,16,512]{3,2,1,0:T(8,128)(2,1)S(1)}, bf16[4,4,16,512]{3,2,1,0:T(8,128)(2,1)S(1)}, u32[]{:S(2)}, u32[]{:S(2)}) collective-permute-start(bf16[4,4,16,512]{3,2,1,0:T(8,128)(2,1)S(1)} %pad_maximum_fusion.3), channel_id=1, source_target_pairs={{0,4},{1,5},{2,6},{3,7},{4,0},{5,1},{6,2},{7,3},{8,12},{9,13},{10,... | collective-permute-start | bytes 786440 | tf_op jit(solution)/shard_map/ppermute | solution.py:23
  75.8 5.2 %collective-permute-done.2 = bf16[4,4,16,512]{3,2,1,0:T(8,128)(2,1)S(1)} collective-permute-done((bf16[4,4,16,512]{3,2,1,0:T(8,128)(2,1)S(1)}, bf16[4,4,16,512]{3,2,1,0:T(8,128)(2,1)S(1)}, u32[]{:S(2)}, u32[]{:S(2)}) %collective-permute-start.2) | collective-permute-done | bytes 262176 | tf_op jit(solution)/shard_map/ppermute | solution.py:23
  83.2 10.3 %collective-permute-done.3 = bf16[8,4,16,512]{3,2,1,0:T(8,128)(2,1)} collective-permute-done((bf16[8,4,16,512]{3,2,1,0:T(8,128)(2,1)S(1)}, bf16[8,4,16,512]{3,2,1,0:T(8,128)(2,1)}, u32[]{:S(2)}, u32[]{:S(2)}) %collective-permute-start.3) | collective-permute-done | bytes 524320 | tf_op jit(solution)/shard_map/ppermute | solution.py:23
  95.7 2.7 %collective-permute-start.4 = (bf16[16,4,16,512]{3,2,1,0:T(8,128)(2,1)}, bf16[16,4,16,512]{3,2,1,0:T(8,128)(2,1)}, u32[]{:S(2)}, u32[]{:S(2)}) collective-permute-start(bf16[16,4,16,512]{3,2,1,0:T(8,128)(2,1)} %pad_maximum_fusion.1), channel_id=1, source_target_pairs={{0,16},{1,17},{2,18},{3,19},{4,20},{5,21},{6,22},{7,23},{8,24},{9,... | collective-permute-start | bytes 3145736 | tf_op jit(solution)/shard_map/ppermute | solution.py:23
  98.5 2.4 copy.79
  100.9 18.4 %collective-permute-done.4 = bf16[16,4,16,512]{3,2,1,0:T(8,128)(2,1)} collective-permute-done((bf16[16,4,16,512]{3,2,1,0:T(8,128)(2,1)}, bf16[16,4,16,512]{3,2,1,0:T(8,128)(2,1)}, u32[]{:S(2)}, u32[]{:S(2)}) %collective-permute-start.4) | collective-permute-done | bytes 1048608 | tf_op jit(solution)/shard_map/ppermute | solution.py:23
  124.5 3.6 %all-to-all-start.1 = ((f32[8,128,224]{1,2,0:T(8,128)}), f32[8,128,224]{1,2,0:T(8,128)S(1)}, u32[]{:S(2)}, u32[]{:S(2)}) async-start(f32[8,128,224]{1,2,0:T(8,128)} %broadcast_in_dim.63), calls=%async_computation.1 | async-start | bytes 1835008 | tf_op jit(solution)/shard_map/all_to_all | solution.py:57
  128.5 9.0 %reduce-window.6 = s32[32,8,128]{2,1,0:T(8,128)S(1)} reduce-window(s32[32,8,128]{2,1,0:T(8,128)S(1)} %fusion.33, s32[]{:T(128)} %constant.31.clone.1), window={size=1x1x128 pad=0_0x0_0x127_0}, to_apply=%region_0.1 | reduce-window | flops 4161536 | bytes 262148 | tf_op jit(solution)/shard_map/reduce-window
  138.3 4.3 %scatter_custom_fusion = s32[2048]{0:T(1024)S(1)} fusion(s32[1024]{0:T(1024)S(1)} %bitcast.86, s32[1024]{0:T(1024)S(1)} %add_select_fusion, s32[]{:T(128)} %constant.28.clone.1), kind=kCustom, calls=%fused_computation.79 | custom fusion | bytes 8196 | tf_op jit(solution)/shard_map/scatter | solution.py:73
  142.6 8.4 %all-to-all-done.1 = f32[8,128,224]{1,2,0:T(8,128)S(1)} async-done(((f32[8,128,224]{1,2,0:T(8,128)}), f32[8,128,224]{1,2,0:T(8,128)S(1)}, u32[]{:S(2)}, u32[]{:S(2)}) %all-to-all-start.1) | async-done | bytes 917536 | tf_op jit(solution)/shard_map/all_to_all | solution.py:57
  151.2 9.0 %gather_fusion = bf16[2048,224]{1,0:T(8,128)(2,1)} fusion(bf16[129,224]{1,0:T(8,128)(2,1)S(1)} %concatenate.34, s32[2048]{0:T(1024)S(1)} %fusion.42), kind=kCustom, calls=%fused_computation | custom fusion | bytes 1843200 | tf_op jit(solution)/shard_map/gather | solution.py:147
  160.2 11.1 %all-to-all-start.2 = ((bf16[32,64,224]{2,1,0:T(8,128)(2,1)}), bf16[32,64,224]{2,1,0:T(8,128)(2,1)S(1)}, u32[]{:S(2)}, u32[]{:S(2)}) async-start(bf16[32,64,224]{2,1,0:T(8,128)(2,1)} %bitcast.80), calls=%async_computation.2 | async-start | bytes 2097152 | tf_op jit(solution)/shard_map/all_to_all | solution.py:148
  171.6 4.3 %scatter_custom_fusion.1 = f32[2048]{0:T(1024)S(1)} fusion(s32[1024]{0:T(1024)S(1)} %bitcast.87, f32[1024]{0:T(1024)S(1)} %reshape.232, f32[]{:T(128)} %constant.27.clone.1), kind=kCustom, calls=%fused_computation.76 | custom fusion | bytes 8196 | tf_op jit(solution)/shard_map/scatter | solution.py:75
  176.0 3.9 %copy.78 = bf16[7168,128]{1,0:T(8,128)(2,1)} copy(bf16[7168,128]{0,1:T(8,128)(2,1)} %bitcast.82) | data formatting | bytes 3670016 | tf_op jit(solution)/shard_map/enf,efd->end/dot_general | solution.py:158
  180.0 8.3 %all-to-all-done.2 = bf16[32,64,224]{2,1,0:T(8,128)(2,1)S(1)} async-done(((bf16[32,64,224]{2,1,0:T(8,128)(2,1)}), bf16[32,64,224]{2,1,0:T(8,128)(2,1)S(1)}, u32[]{:S(2)}, u32[]{:S(2)}) %all-to-all-start.2) | async-done | bytes 917536 | tf_op jit(solution)/shard_map/all_to_all | solution.py:148
  190.5 2.6 convert_element_type.70
  195.1 4.4 %multiply_bitcast_fusion = f32[8,64,896]{2,1,0:T(8,128)} fusion(bf16[8,896,128]{2,1,0:T(8,128)(2,1)} %bitcast.78, f32[64]{0:T(128)S(1)} %dynamic_slice.10, bf16[64,7168]{1,0:T(8,128)(2,1)S(1)} %convert_element_type.70, bf16[1,7168,128]{2,1,0:T(8,128)(2,1)} %param.22, f32[64,128]{1,0:T(8,128)S(1)} %fusion.5), kind=kOutput, calls=%fused_computation.14 | convolution fusion | flops 235388928 | bytes 6455552 | tf_op jit(solution)/shard_map/enf,efd->end/dot_general | solution.py:158
  199.6 4.3 %all-to-all-start.3 = ((f32[8,64,896]{2,1,0:T(8,128)}), f32[8,64,896]{2,1,0:T(8,128)}, u32[]{:S(2)}, u32[]{:S(2)}) async-start(f32[8,64,896]{2,1,0:T(8,128)} %multiply_bitcast_fusion), calls=%async_computation.3 | async-start | bytes 3670016 | tf_op jit(solution)/shard_map/all_to_all | solution.py:39
  204.0 43.1 %all-to-all-done.3 = f32[8,64,896]{2,1,0:T(8,128)} async-done(((f32[8,64,896]{2,1,0:T(8,128)}), f32[8,64,896]{2,1,0:T(8,128)}, u32[]{:S(2)}, u32[]{:S(2)}) %all-to-all-start.3) | async-done | bytes 1835040 | tf_op jit(solution)/shard_map/all_to_all | solution.py:39
  251.4 17.2 %all_to_all.30 = f32[32,4,896]{2,1,0:T(4,128)S(1)} all-to-all(f32[32,4,896]{2,1,0:T(4,128)S(1)} %reshape.209), channel_id=1, replica_groups=mesh['ctx'=8,'exp'=32] {'exp'}, dimensions={0} | all-to-all | bytes 917504 | tf_op jit(solution)/shard_map/all_to_all | solution.py:39
  (83 shorter events, 34.2 us)
Async XLA Ops:
  0.0 1.6 copy-start
  0.0 3.5 %copy-start.3 = (bf16[4,64,128]{2,1,0:T(8,128)(2,1)S(1)}, bf16[4,64,128]{2,1,0:T(8,128)(2,1)}, u32[]{:S(2)}) copy-start(bf16[4,64,128]{2,1,0:T(8,128)(2,1)} %param.14) | copy-start | bytes 196612
  0.0 3.5 %copy-start.2 = (bf16[4,64,512]{2,1,0:T(8,128)(2,1)S(1)}, bf16[4,64,512]{2,1,0:T(8,128)(2,1)}, u32[]{:S(2)}) copy-start(bf16[4,64,512]{2,1,0:T(8,128)(2,1)} %param.16) | copy-start | bytes 786436
  59.3 7.6 %collective-permute-start = (bf16[1,4,16,512]{3,2,1,0:T(8,128)(2,1)S(1)}, bf16[1,4,16,512]{3,2,1,0:T(8,128)(2,1)S(1)}, u32[]{:S(2)}, u32[]{:S(2)}) collective-permute-start(bf16[1,4,16,512]{3,2,1,0:T(8,128)(2,1)S(1)} %fusion.35), channel_id=1, source_target_pairs={{0,1},{1,0},{2,3},{3,2},{4,5},{5,4},{6,7},{7,6},{8,9},{9,8},{10,11... | collective-permute-start | bytes 196616 | tf_op jit(solution)/shard_map/ppermute | solution.py:23
  68.0 4.8 %collective-permute-start.1 = (bf16[2,4,16,512]{3,2,1,0:T(8,128)(2,1)S(1)}, bf16[2,4,16,512]{3,2,1,0:T(8,128)(2,1)S(1)}, u32[]{:S(2)}, u32[]{:S(2)}) collective-permute-start(bf16[2,4,16,512]{3,2,1,0:T(8,128)(2,1)S(1)} %pad_maximum_fusion.4), channel_id=1, source_target_pairs={{0,2},{1,3},{2,0},{3,1},{4,6},{5,7},{6,4},{7,5},{8,10},{9,11},{10,... | collective-permute-start | bytes 393224 | tf_op jit(solution)/shard_map/ppermute | solution.py:23
  72.8 8.2 %collective-permute-start.2 = (bf16[4,4,16,512]{3,2,1,0:T(8,128)(2,1)S(1)}, bf16[4,4,16,512]{3,2,1,0:T(8,128)(2,1)S(1)}, u32[]{:S(2)}, u32[]{:S(2)}) collective-permute-start(bf16[4,4,16,512]{3,2,1,0:T(8,128)(2,1)S(1)} %pad_maximum_fusion.3), channel_id=1, source_target_pairs={{0,4},{1,5},{2,6},{3,7},{4,0},{5,1},{6,2},{7,3},{8,12},{9,13},{10,... | collective-permute-start | bytes 786440 | tf_op jit(solution)/shard_map/ppermute | solution.py:23
  81.1 0.7 copy-start.1
  81.9 11.6 %collective-permute-start.3 = (bf16[8,4,16,512]{3,2,1,0:T(8,128)(2,1)S(1)}, bf16[8,4,16,512]{3,2,1,0:T(8,128)(2,1)}, u32[]{:S(2)}, u32[]{:S(2)}) collective-permute-start(bf16[8,4,16,512]{3,2,1,0:T(8,128)(2,1)S(1)} %pad_maximum_fusion.2), channel_id=1, source_target_pairs={{0,8},{1,9},{2,10},{3,11},{4,12},{5,13},{6,14},{7,15},{8,0},{9,1},... | collective-permute-start | bytes 1572872 | tf_op jit(solution)/shard_map/ppermute | solution.py:23
  95.7 23.6 %collective-permute-start.4 = (bf16[16,4,16,512]{3,2,1,0:T(8,128)(2,1)}, bf16[16,4,16,512]{3,2,1,0:T(8,128)(2,1)}, u32[]{:S(2)}, u32[]{:S(2)}) collective-permute-start(bf16[16,4,16,512]{3,2,1,0:T(8,128)(2,1)} %pad_maximum_fusion.1), channel_id=1, source_target_pairs={{0,16},{1,17},{2,18},{3,19},{4,20},{5,21},{6,22},{7,23},{8,24},{9,... | collective-permute-start | bytes 3145736 | tf_op jit(solution)/shard_map/ppermute | solution.py:23
  123.5 4.6 %copy-start.5 = (s32[128,8]{0,1:T(8,128)S(1)}, s32[128,8]{0,1:T(8,128)}, u32[]{:S(2)}) copy-start(s32[128,8]{0,1:T(8,128)} %param.24) | copy-start | bytes 12292
  123.5 4.9 %copy-start.4 = (bf16[128,224]{0,1:T(8,128)(2,1)S(1)}, bf16[128,224]{0,1:T(8,128)(2,1)}, u32[]{:S(2)}) copy-start(bf16[128,224]{0,1:T(8,128)(2,1)} %param.19) | copy-start | bytes 172036
  124.5 26.5 %all-to-all-start.1 = ((f32[8,128,224]{1,2,0:T(8,128)}), f32[8,128,224]{1,2,0:T(8,128)S(1)}, u32[]{:S(2)}, u32[]{:S(2)}) async-start(f32[8,128,224]{1,2,0:T(8,128)} %broadcast_in_dim.63), calls=%async_computation.1 | async-start | bytes 1835008 | tf_op jit(solution)/shard_map/all_to_all | solution.py:57
  160.2 11.1 %copy-start.6 = (bf16[7168]{0:T(1024)(128)(2,1)S(1)}, bf16[7168]{0:T(1024)(128)(2,1)}, u32[]{:S(2)}) copy-start(bf16[7168]{0:T(1024)(128)(2,1)} %param.20) | copy-start | bytes 43012
  160.2 11.2 %copy-start.7 = (f32[128,8]{0,1:T(8,128)S(1)}, f32[128,8]{0,1:T(8,128)}, u32[]{:S(2)}) copy-start(f32[128,8]{0,1:T(8,128)} %param.25) | copy-start | bytes 12292
  160.2 28.0 %all-to-all-start.2 = ((bf16[32,64,224]{2,1,0:T(8,128)(2,1)}), bf16[32,64,224]{2,1,0:T(8,128)(2,1)S(1)}, u32[]{:S(2)}, u32[]{:S(2)}) async-start(bf16[32,64,224]{2,1,0:T(8,128)(2,1)} %bitcast.80), calls=%async_computation.2 | async-start | bytes 2097152 | tf_op jit(solution)/shard_map/all_to_all | solution.py:148
  199.6 47.5 %all-to-all-start.3 = ((f32[8,64,896]{2,1,0:T(8,128)}), f32[8,64,896]{2,1,0:T(8,128)}, u32[]{:S(2)}, u32[]{:S(2)}) async-start(f32[8,64,896]{2,1,0:T(8,128)} %multiply_bitcast_fusion), calls=%async_computation.3 | async-start | bytes 3670016 | tf_op jit(solution)/shard_map/all_to_all | solution.py:39
